TPU v7x, 128 devices: a whole 4x4x4 slice. The times are simulated.
128 devices in a mesh: dp: 8 (over z, core), mp: 16 (over y, x).
Axes of the slice: x: 4, y: 4, z: 4, core: 2. Of those that a mesh axis runs over, the one named last changes fastest.
Arguments:
- crop_hidden: bfloat16 [8, 1536, 8192], P(None, 'dp', 'mp'), may hold values from -15 to 15
- projector_weight: bfloat16 [8192, 8192], P('mp'), may hold values from -0.21213203 to 0.21213203
- pairing: int32 [8, 1536], P(None, 'dp'), may hold values from 0 to 191, as said below
Outputs:
- embeddings: float32 [8192, 8, 1536], P('mp', 'dp')
- loss_terms: float32 [4], replicated
Inputs may be any that keep to these rules, and one draw needn't show every extreme that they name: Each aligned block of 192 entries of a row of pairing is a permutation of 0 to 191.
All inputs are finite; a program needn't handle non-finite values.
Results may differ from a plain program's by a relative error of at most 0.0003.
Values may be sent and summed in bfloat16 or wider, within the bound.
No kernel may reach another device: no remote copies, remote signals or barrier semaphores. Data moves between devices by JAX's collectives and lax.ppermute only.
A program may use at most 128 MiB of HBM per device.

v0:
```python
import functools
import jax
import jax.numpy as jnp
from jax import lax
from jax.sharding import Mesh
from jax.sharding import PartitionSpec as P

MP = ("mp_0", "mp_1")
DP = ("dp_0", "dp_1")
DP_MP = ("dp_0", "dp_1", "mp_0", "mp_1")
highest = lax.Precision.HIGHEST
epsilon = 0.0001


def by_axis(x, axes):
    return functools.reduce(lax.psum, axes, x)


def local(crop_hidden, projector_weight, pairing):
    crop_count, local_rows, width_part = crop_hidden.shape
    features = projector_weight.shape[1]
    total_rows = crop_count * local_rows
    column_block = lax.all_to_all(projector_weight, MP, split_axis=1, concat_axis=0, tiled=True)
    shards = lax.all_gather(crop_hidden, MP, axis=2, tiled=True)
    flat_piece = shards.reshape(total_rows, shards.shape[2])
    embedded = lax.dot_general(
        column_block, flat_piece, (((0,), (1,)), ((), ())), preferred_element_type=jnp.float32
    )
    feature_part = embedded.shape[0]
    by_crop = embedded.reshape(feature_part, crop_count, local_rows)
    onehot = (pairing[:, :, None] == jnp.arange(local_rows, dtype=jnp.int32)[None, None, :]).astype(
        jnp.float32
    )
    aligned = jnp.einsum("jcr,cri->jci", by_crop, onehot, precision=highest)
    invariance = 0.0
    for anchor in range(2):
        differ = aligned - aligned[:, anchor : anchor + 1, :]
        invariance = invariance + jnp.sum(differ * differ)
    owned_block = lax.all_to_all(by_crop, DP, split_axis=1, concat_axis=2, tiled=True)
    batch_rows = owned_block.shape[2]
    column_mean = jnp.mean(owned_block, axis=2, keepdims=True)
    centered = owned_block - column_mean
    variance = jnp.sum(centered * centered, axis=2) / (batch_rows - 1)
    hinge_sum = jnp.sum(jax.nn.relu(1.0 - jnp.sqrt(variance + epsilon)))
    diagonal_sq = jnp.sum(variance * variance)
    gram_scale = 1.0 / ((batch_rows - 1) * (batch_rows - 1))
    partial_gram = jnp.einsum("jcr,jcs->crs", centered, centered, precision=highest)
    gram_block = lax.psum(partial_gram.astype(jnp.bfloat16), MP).astype(jnp.float32)
    frobenius = jnp.where(
        lax.axis_index(MP) == 0, jnp.sum(gram_block * gram_block) * gram_scale, 0.0
    )
    totals = (
        by_axis(invariance, DP_MP),
        by_axis(hinge_sum, DP_MP),
        by_axis(frobenius - diagonal_sq, DP_MP),
    )
    invariance_loss = totals[0] / (2 * (crop_count - 1) * batch_rows * features)
    variance_loss = totals[1] / (crop_count * features)
    covariance_loss = totals[2] / (crop_count * features)
    total_loss = 25.0 * invariance_loss + 25.0 * variance_loss + covariance_loss
    loss_terms = jnp.stack([invariance_loss, variance_loss, covariance_loss, total_loss])
    return (owned_block, loss_terms)


def solution(mesh):
    torus = Mesh(mesh.devices.reshape(4, 2, 4, 4), ("dp_0", "dp_1", "mp_0", "mp_1"))
    placed = (P(None, DP, MP), P(MP, None), P(None, DP))
    return jax.shard_map(
        local, mesh=torus, in_specs=placed, out_specs=(P(MP, DP, None), P()), check_vma=False
    )
```

profile of v0, /device:TPU:0, one launch (start us, length us, event | category | flops | bytes accessed | tf_op | source)
XLA Modules:
  0.0 498.9 jit_solution(17605152332946094416)
XLA Ops:
  7.2 0.0 all-gather.2.cloned.1.call-start
  7.2 0.7 all-gather.2.cloned.1.call-update
  7.9 0.0 all-reduce.6.cloned.1.call-start
  7.9 7.5 %copy.9 = bf16[64,16,8,512]{3,2,0,1:T(8,128)(2,1)} copy(bf16[64,16,8,512]{3,2,1,0:T(8,128)(2,1)} %bitcast.30) | data formatting | bytes 16777216 | tf_op jit(solution)/shard_map/all_to_all | solution.py:23
  15.4 128.3 %all_to_all.31 = bf16[512,16,512]{2,0,1:T(8,128)(2,1)} all-to-all(bf16[512,16,512]{2,0,1:T(8,128)(2,1)} %bitcast.29), channel_id=1, replica_groups=mesh['dp_0'=4,'dp_1'=2,'mp_0'=4,'mp_1'=4] {'mp_0','mp_1'}, dimensions={1} | all-to-all | bytes 16777216 | tf_op jit(solution)/shard_map/all_to_all | solution.py:23
  143.8 117.0 %all-gather.2.cloned.1.call-done = bf16[8,192,8192]{2,1,0:T(8,128)(2,1)} async-done(((bf16[8,192,512]{2,1,0:T(8,128)(2,1)}), bf16[8,192,8192]{2,1,0:T(8,128)(2,1)}) %all-gather.2.cloned.1.call-update) | async-done | bytes 25165840 | tf_op jit(solution)/shard_map/all_gather | solution.py:24
  260.8 18.9 %fusion.2 = f32[512,8,192]{0,2,1:T(8,128)S(1)} fusion(bf16[8192,512,1]{1,0,2:T(8,128)(2,1)} %bitcast.31, bf16[8,192,8192]{2,1,0:T(8,128)(2,1)} %all-gather.2.cloned.1.call-done), kind=kOutput, calls=%fused_computation.17 | convolution fusion | flops 12884901888 | bytes 36700160 | tf_op jit(solution)/shard_map/dot_general | solution.py:26
  279.7 0.0 copy-start
  279.7 1.7 copy-done
  281.3 42.7 %all_to_all.32 = f32[512,8,192]{0,2,1:T(8,128)S(1)} all-to-all(f32[512,8,192]{0,2,1:T(8,128)S(1)} %fusion.2), channel_id=1, replica_groups=mesh['dp_0'=4,'dp_1'=2,'mp_0'=4,'mp_1'=4] {'dp_0','dp_1'}, dimensions={1} | all-to-all | bytes 6291456 | tf_op jit(solution)/shard_map/all_to_all | solution.py:39
  324.0 0.3 reduce_sum.65
  324.3 0.6 multiply_reduce_fusion.1
  324.8 16.8 %fusion = bf16[1,1536,1536]{2,1,0:T(8,128)(2,1)} fusion(f32[512,1536]{0,1:T(8,128)S(1)} %bitcast.32), kind=kOutput, calls=%fused_computation.3 | convolution fusion | flops 14497873920 | bytes 7864320 | tf_op jit(solution)/shard_map/jcr,jcs->crs/dot_general | solution.py:47
  341.6 0.0 copy-start.1
  341.6 0.0 all-reduce.6.cloned.1.call-update
  341.6 0.7 copy-done.1
  342.3 3.9 convolution_bitcast_fusion
  346.2 0.1 slice_bitcast_fusion.1
  346.2 2.0 multiply_reduce_fusion.2
  349.5 5.4 %copy.6 = f32[512,1,1536]{2,1,0:T(1,128)} copy(f32[512,1,1536]{0,2,1:T(8,128)S(1)} %bitcast.28) | data formatting | bytes 6291456
  354.9 0.7 multiply_reduce_fusion.4
  355.6 91.4 %all-reduce.6.cloned.1.call-done = bf16[1,1536,1536]{2,1,0:T(8,128)(2,1)} async-done(((bf16[1,1536,1536]{2,1,0:T(8,128)(2,1)}), bf16[1,1536,1536]{2,1,0:T(8,128)(2,1)}) %all-reduce.6.cloned.1.call-update) | async-done | bytes 4718608 | tf_op jit(solution)/shard_map/psum | solution.py:48
  447.0 5.3 %multiply_reduce_fusion = f32[]{:T(128)} fusion(bf16[1,1536,1536]{2,1,0:T(8,128)(2,1)} %all-reduce.6.cloned.1.call-done), kind=kLoop, calls=%fused_computation | loop fusion | flops 7077887 | bytes 4718596 | tf_op jit(solution)/shard_map/reduce_sum | solution.py:50
  453.5 11.3 %all-reduce.2 = (f32[]{:T(128)}, f32[]{:T(128)}, f32[]{:T(128)}) all-reduce(f32[]{:T(128)S(6)} %add.47, f32[]{:T(128)} %get-tuple-element.7, f32[]{:T(128)S(6)} %sub.61), channel_id=1, replica_groups=mesh['dp_0'=4,'dp_1'=2,'mp_0'=4,'mp_1'=4] {'dp_0'}, use_global_device_ids=true, to_apply=%region_2.0 | all-reduce | flops 3 | bytes 24 | tf_op jit(solution)/shard_map/psum | solution.py:16
  464.8 3.2 all-reduce.3
  467.9 11.0 %all-reduce.1 = (f32[]{:T(128)}, f32[]{:T(128)}, f32[]{:T(128)}) all-reduce(f32[]{:T(128)} %get-tuple-element.17, f32[]{:T(128)} %get-tuple-element.18, f32[]{:T(128)} %get-tuple-element.19), channel_id=1, replica_groups=mesh['dp_0'=4,'dp_1'=2,'mp_0'=4,'mp_1'=4] {'mp_0'}, use_global_device_ids=true, to_apply=%region_4.5 | all-reduce | flops 3 | bytes 24 | tf_op jit(solution)/shard_map/psum | solution.py:16
  478.9 9.4 %all-reduce = (f32[]{:T(128)}, f32[]{:T(128)}, f32[]{:T(128)}) all-reduce(f32[]{:T(128)} %get-tuple-element.11, f32[]{:T(128)} %get-tuple-element.12, f32[]{:T(128)} %get-tuple-element.13), channel_id=1, replica_groups=mesh['dp_0'=4,'dp_1'=2,'mp_0'=4,'mp_1'=4] {'mp_1'}, use_global_device_ids=true, to_apply=%region_5.6 | all-reduce | flops 3 | bytes 24 | tf_op jit(solution)/shard_map/psum | solution.py:16
  491.5 0.6 pad_maximum_fusion
  (1 shorter events, 0.0 us)
Async XLA Ops:
  7.2 253.6 %all-gather.2.cloned.1.call-start = ((), (), s32[]{:S(2)}) async-start(), calls=%async_computation.2 | async-start | bytes 26738688 | tf_op jit(solution)/shard_map/all_gather | solution.py:24
  7.9 439.1 %all-reduce.6.cloned.1.call-start = ((), (), s32[]{:S(2)}) async-start(), calls=%async_computation.3 | async-start | bytes 9437184 | tf_op jit(solution)/shard_map/psum | solution.py:48
  279.7 1.7 copy-start
  341.6 0.7 copy-start.1
Sparse Core Ops, SparseCore 0:
  10.1 250.6 all-gather.1
  341.7 105.2 all-reduce.5
where the time goes:
time: 499 us
  waiting for transfers between devices  209 us (42%)
  blocking collectives  206 us (41%)
  matrix products  39.5 us (8%)
  between operations  19.8 us (4%)
  local copies, waits for them, and re-layouts  15.3 us (3%)
  other arithmetic  9.4 us (2%)
    all_to_all x1, blocking collectives, local(): lax.all_to_all(projector_weight, MP, split_axis=1, concat_axis=0, tiled=T...  128 us
    all_gather x1, waiting for transfers between devices, local(): shards = lax.all_gather(crop_hidden, MP, axis=2, tiled=True)  117 us
    psum x1, waiting for transfers between devices, local(): lax.psum(partial_gram.astype(jnp.bfloat16), MP).astype(jnp.float32)  91.4 us
    all_to_all x1, blocking collectives, local(): lax.all_to_all(by_crop, DP, split_axis=1, concat_axis=2, tiled=True)  42.7 us
    psum x4, blocking collectives, by_axis(): return functools.reduce(lax.psum, axes, x)  34.8 us
    dot_general x1, matrix products, local(): lax.dot_general(column_block, flat_piece, (((0,), (1,)), ((), ())), prefe...  18.9 us
    dot_general x1, matrix products, local(): jnp.einsum('jcr,jcs->crs', centered, centered, precision=highest)  16.8 us
  transfers between devices with their start and end apart: 2, of which 2 were waited for; matrix products, arithmetic and copies ran while one was open for 4% of the time, Pallas kernels for 0%

commit v1 on v0

--- a/solution.py
+++ b/solution.py
@@ -45,7 +45,9 @@
     diagonal_sq = jnp.sum(variance * variance)
     gram_scale = 1.0 / ((batch_rows - 1) * (batch_rows - 1))
     partial_gram = jnp.einsum("jcr,jcs->crs", centered, centered, precision=highest)
-    gram_block = lax.psum(partial_gram.astype(jnp.bfloat16), MP).astype(jnp.float32)
+    gram_block = lax.psum(lax.psum(partial_gram.astype(jnp.bfloat16), "mp_0"), "mp_1").astype(
+        jnp.float32
+    )
     frobenius = jnp.where(
         lax.axis_index(MP) == 0, jnp.sum(gram_block * gram_block) * gram_scale, 0.0
     )

time: 499 us -> 596 us (1.19)
  waiting for transfers between devices: 209 us -> 306 us
    psum x1 -> x2, waiting for transfers between devices: 91.4 us -> 189 us  [the longest x1 98.6 us: local(): lax.psum(partial_gram.astype(jnp.bfloat16), 'mp_0')]
  transfers between devices with their start and end apart: 2 -> 3, of which waited for: 2 -> 3; matrix products, arithmetic and copies ran while one was open for 4% -> 3% of each run, Pallas kernels for 0% -> 0%
where the time goes in v1:
time: 596 us
  waiting for transfers between devices  306 us (51%)
  blocking collectives  206 us (35%)
  matrix products  39.5 us (7%)
  between operations  19.7 us (3%)
  local copies, waits for them, and re-layouts  14.6 us (2%)
  other arithmetic  9.51 us (2%)
    all_to_all x1, blocking collectives, local(): lax.all_to_all(projector_weight, MP, split_axis=1, concat_axis=0, tiled=T...  128 us
    all_gather x1, waiting for transfers between devices, local(): shards = lax.all_gather(crop_hidden, MP, axis=2, tiled=True)  117 us
    psum x1, waiting for transfers between devices, local(): lax.psum(partial_gram.astype(jnp.bfloat16), 'mp_0')  98.6 us
    psum x1, waiting for transfers between devices, local(): lax.psum(lax.psum(partial_gram.astype(jnp.bfloat16), 'mp_0'), 'mp_1')  90.1 us
    all_to_all x1, blocking collectives, local(): lax.all_to_all(by_crop, DP, split_axis=1, concat_axis=2, tiled=True)  42.7 us
    psum x4, blocking collectives, by_axis(): return functools.reduce(lax.psum, axes, x)  34.8 us
    dot_general x1, matrix products, local(): lax.dot_general(column_block, flat_piece, (((0,), (1,)), ((), ())), prefe...  18.9 us
    dot_general x1, matrix products, local(): jnp.einsum('jcr,jcs->crs', centered, centered, precision=highest)  16.8 us
  transfers between devices with their start and end apart: 3, of which 3 were waited for; matrix products, arithmetic and copies ran while one was open for 3% of the time, Pallas kernels for 0%

profile of v1, /device:TPU:0, one launch (start us, length us, event | category | flops | bytes accessed | tf_op | source)
XLA Modules:
  0.0 595.9 jit_solution(11724488774731935560)
XLA Ops:
  7.2 0.0 all-gather.2.cloned.1.call-start
  7.2 0.7 all-gather.2.cloned.1.call-update
  7.9 0.0 all-reduce.7.cloned.1.call-start
  7.9 7.5 %copy.9 = bf16[64,16,8,512]{3,2,0,1:T(8,128)(2,1)} copy(bf16[64,16,8,512]{3,2,1,0:T(8,128)(2,1)} %bitcast.30) | data formatting | bytes 16777216 | tf_op jit(solution)/shard_map/all_to_all | solution.py:23
  15.4 128.3 %all_to_all.31 = bf16[512,16,512]{2,0,1:T(8,128)(2,1)} all-to-all(bf16[512,16,512]{2,0,1:T(8,128)(2,1)} %bitcast.29), channel_id=1, replica_groups=mesh['dp_0'=4,'dp_1'=2,'mp_0'=4,'mp_1'=4] {'mp_0','mp_1'}, dimensions={1} | all-to-all | bytes 16777216 | tf_op jit(solution)/shard_map/all_to_all | solution.py:23
  143.8 117.0 %all-gather.2.cloned.1.call-done = bf16[8,192,8192]{2,1,0:T(8,128)(2,1)} async-done(((bf16[8,192,512]{2,1,0:T(8,128)(2,1)}), bf16[8,192,8192]{2,1,0:T(8,128)(2,1)}) %all-gather.2.cloned.1.call-update) | async-done | bytes 25165840 | tf_op jit(solution)/shard_map/all_gather | solution.py:24
  260.8 18.9 %fusion.2 = f32[512,8,192]{0,2,1:T(8,128)S(1)} fusion(bf16[8192,512,1]{1,0,2:T(8,128)(2,1)} %bitcast.31, bf16[8,192,8192]{2,1,0:T(8,128)(2,1)} %all-gather.2.cloned.1.call-done), kind=kOutput, calls=%fused_computation.17 | convolution fusion | flops 12884901888 | bytes 36700160 | tf_op jit(solution)/shard_map/dot_general | solution.py:26
  279.7 0.0 copy-start
  279.7 1.7 copy-done
  281.3 42.7 %all_to_all.32 = f32[512,8,192]{0,2,1:T(8,128)S(1)} all-to-all(f32[512,8,192]{0,2,1:T(8,128)S(1)} %fusion.2), channel_id=1, replica_groups=mesh['dp_0'=4,'dp_1'=2,'mp_0'=4,'mp_1'=4] {'dp_0','dp_1'}, dimensions={1} | all-to-all | bytes 6291456 | tf_op jit(solution)/shard_map/all_to_all | solution.py:39
  324.0 0.3 reduce_sum.65
  324.3 0.6 multiply_reduce_fusion.1
  324.8 16.8 %fusion = bf16[1,1536,1536]{2,1,0:T(8,128)(2,1)} fusion(f32[512,1536]{0,1:T(8,128)S(1)} %bitcast.32), kind=kOutput, calls=%fused_computation.3 | convolution fusion | flops 14497873920 | bytes 7864320 | tf_op jit(solution)/shard_map/jcr,jcs->crs/dot_general | solution.py:47
  341.6 0.0 all-reduce.7.cloned.1.call-update
  341.6 0.0 copy-start.1
  341.6 0.2 all-reduce.9.cloned.1.call-start
  341.8 98.6 %all-reduce.7.cloned.1.call-done = bf16[1,1536,1536]{2,1,0:T(8,128)(2,1)} async-done(((bf16[1,1536,1536]{2,1,0:T(8,128)(2,1)}), bf16[1,1536,1536]{2,1,0:T(8,128)(2,1)}) %all-reduce.7.cloned.1.call-update) | async-done | bytes 4718608 | tf_op jit(solution)/shard_map/psum | solution.py:48
  440.5 0.0 all-reduce.9.cloned.1.call-update
  440.5 0.0 copy-done.1
  440.5 3.9 convolution_bitcast_fusion
  444.4 0.1 slice_bitcast_fusion.1
  444.5 2.0 multiply_reduce_fusion.2
  447.8 5.4 copy.6
  453.2 0.7 multiply_reduce_fusion.4
  453.8 90.1 %all-reduce.9.cloned.1.call-done = bf16[1,1536,1536]{2,1,0:T(8,128)(2,1)} async-done(((bf16[1,1536,1536]{2,1,0:T(8,128)(2,1)}), bf16[1,1536,1536]{2,1,0:T(8,128)(2,1)}) %all-reduce.9.cloned.1.call-update) | async-done | bytes 4718608 | tf_op jit(solution)/shard_map/psum | solution.py:48
  544.0 5.4 multiply_reduce_fusion
  550.8 11.3 %all-reduce.2 = (f32[]{:T(128)}, f32[]{:T(128)}, f32[]{:T(128)}) all-reduce(f32[]{:T(128)S(6)} %add.49, f32[]{:T(128)} %get-tuple-element.7, f32[]{:T(128)S(6)} %sub.61), channel_id=1, replica_groups=mesh['dp_0'=4,'dp_1'=2,'mp_0'=4,'mp_1'=4] {'dp_0'}, use_global_device_ids=true, to_apply=%region_2.0 | all-reduce | flops 3 | bytes 24 | tf_op jit(solution)/shard_map/psum | solution.py:16
  562.0 3.2 all-reduce.3
  565.2 11.1 %all-reduce.1 = (f32[]{:T(128)}, f32[]{:T(128)}, f32[]{:T(128)}) all-reduce(f32[]{:T(128)} %get-tuple-element.17, f32[]{:T(128)} %get-tuple-element.18, f32[]{:T(128)} %get-tuple-element.19), channel_id=1, replica_groups=mesh['dp_0'=4,'dp_1'=2,'mp_0'=4,'mp_1'=4] {'mp_0'}, use_global_device_ids=true, to_apply=%region_4.5 | all-reduce | flops 3 | bytes 24 | tf_op jit(solution)/shard_map/psum | solution.py:16
  576.3 9.3 %all-reduce = (f32[]{:T(128)}, f32[]{:T(128)}, f32[]{:T(128)}) all-reduce(f32[]{:T(128)} %get-tuple-element.11, f32[]{:T(128)} %get-tuple-element.12, f32[]{:T(128)} %get-tuple-element.13), channel_id=1, replica_groups=mesh['dp_0'=4,'dp_1'=2,'mp_0'=4,'mp_1'=4] {'mp_1'}, use_global_device_ids=true, to_apply=%region_5.6 | all-reduce | flops 3 | bytes 24 | tf_op jit(solution)/shard_map/psum | solution.py:16
  588.8 0.6 pad_maximum_fusion
  (1 shorter events, 0.0 us)
Async XLA Ops:
  7.2 253.6 %all-gather.2.cloned.1.call-start = ((), (), s32[]{:S(2)}) async-start(), calls=%async_computation.2 | async-start | bytes 26738688 | tf_op jit(solution)/shard_map/all_gather | solution.py:24
  7.9 432.6 %all-reduce.7.cloned.1.call-start = ((), (), s32[]{:S(2)}) async-start(), calls=%async_computation.3 | async-start | bytes 9437184 | tf_op jit(solution)/shard_map/psum | solution.py:48
  279.7 1.7 copy-start
  341.6 98.9 %copy-start.1 = (s32[8,192]{1,0:T(8,128)S(1)}, s32[8,192]{1,0:T(8,128)}, u32[]{:S(2)}) copy-start(s32[8,192]{1,0:T(8,128)} %param.5) | copy-start | bytes 18436
  341.6 202.4 %all-reduce.9.cloned.1.call-start = ((), (), s32[]{:S(2)}) async-start(), calls=%async_computation.4 | async-start | bytes 9437184 | tf_op jit(solution)/shard_map/psum | solution.py:48
Sparse Core Ops, SparseCore 0:
  10.1 250.6 all-gather.1
  341.7 98.6 all-reduce.6
  442.8 101.0 all-reduce.8
